TPU v7x, 32 devices: a whole 2x2x4 slice. The times are simulated.
32 devices in a mesh: smp: 8 (over z, y), var: 4 (over x, core).
Axes of the slice: x: 2, y: 2, z: 4, core: 2. Of those that a mesh axis runs over, the one named last changes fastest.
Arguments:
- dosage: int32 [512, 2048], P('smp', 'var'), may hold values from -2147483648 to 2147483647, as said below
- shares_init: float32 [12, 8192], P(None, ('smp', 'var')), may hold values from 0.1 to 1
- freqs_init: float32 [12, 2048], P(None, ('var', 'smp')), may hold values from 0.019 to 0.981
Outputs:
- shares: float32 [12, 8192], P(None, ('smp', 'var'))
- freqs: float32 [12, 2048], P(None, ('var', 'smp'))
Inputs may be any that keep to these rules, and one draw needn't show every extreme that they name: Every 2-bit code in a word of dosage is 0, 1, 2 or 3, and 3 marks a missing genotype.
All inputs are finite; a program needn't handle non-finite values.
Results may differ from a plain program's by a relative error of at most 0.0003.
Values sent between devices are 32-bit elements; how exact they have to be, the bound alone decides.
A program may use at most 64 MiB of HBM per device.

v0:
```python
import jax
import jax.numpy as jnp
from jax import lax
from jax.sharding import PartitionSpec as P

ITERS = 2
HIGH = lax.Precision.HIGHEST


def unpack_codes(packed):
    shifts = 2 * jnp.arange(16, dtype=jnp.int32)
    codes = jnp.bitwise_and(jnp.right_shift(packed[:, None, :], shifts[None, :, None]), 3)
    return codes.reshape(packed.shape[0] * 16, packed.shape[1])


def expect_sums(packed, shares_block, freqs_block):
    codes = unpack_codes(packed)
    live = (codes < 3).astype(jnp.float32)
    allele_f = live * codes.astype(jnp.float32)
    probs = jnp.einsum("kn,km->nm", shares_block, freqs_block, precision=HIGH)
    ratio_alt = allele_f / probs
    ratio_ref = (2.0 * live - allele_f) / (1.0 - probs)
    sum_q = jnp.einsum("km,nm->kn", freqs_block, ratio_alt, precision=HIGH) + jnp.einsum(
        "km,nm->kn", 1.0 - freqs_block, ratio_ref, precision=HIGH
    )
    sum_a = jnp.einsum("kn,nm->km", shares_block, ratio_alt, precision=HIGH)
    sum_b = jnp.einsum("kn,nm->km", shares_block, ratio_ref, precision=HIGH)
    return (sum_q, sum_a, sum_b)


def block_sums(packed, shares_block, freqs_block):
    word_rows = min(packed.shape[0], 16)
    blocks = packed.shape[0] // word_rows
    populations = shares_block.shape[0]
    packed_blocks = packed.reshape(blocks, word_rows, packed.shape[1])
    share_blocks = shares_block.reshape(populations, blocks, word_rows * 16).transpose(1, 0, 2)

    def one_block(carry, items):
        sum_q, sum_a, sum_b = expect_sums(items[0], items[1], freqs_block)
        return ((carry[0] + sum_a, carry[1] + sum_b), sum_q)

    start = (jnp.zeros(freqs_block.shape, jnp.float32), jnp.zeros(freqs_block.shape, jnp.float32))
    totals, sums_q = lax.scan(one_block, start, (packed_blocks, share_blocks))
    sum_q = sums_q.transpose(1, 0, 2).reshape(populations, shares_block.shape[1])
    return (sum_q, totals[0], totals[1])


def renew_shares(shares_block, sum_q):
    numer = shares_block * sum_q
    return (numer + 0.5) / (jnp.sum(numer, axis=0, keepdims=True) + 0.5 * shares_block.shape[0])


def renew_freqs(freqs_block, sum_a, sum_b):
    alt_part = freqs_block * sum_a
    ref_part = (1.0 - freqs_block) * sum_b
    return (alt_part + 0.5) / (alt_part + ref_part + 1.0)


def body(dosage, shares_init, freqs_init):
    own_shares = shares_init / jnp.sum(shares_init, axis=0, keepdims=True)
    own_freqs = freqs_init
    share_width = shares_init.shape[1]
    freq_width = freqs_init.shape[1]
    shares_block = lax.all_gather(own_shares, "var", axis=1, tiled=True)
    freqs_block = lax.all_gather(own_freqs, "smp", axis=1, tiled=True)
    for iteration in range(ITERS):
        part_q, part_a, part_b = block_sums(dosage, shares_block, freqs_block)
        sum_q = lax.psum(part_q, "var")
        sum_a, sum_b = lax.psum((part_a, part_b), "smp")
        shares_block = renew_shares(shares_block, sum_q)
        freqs_block = renew_freqs(freqs_block, sum_a, sum_b)
        if iteration + 1 == ITERS:
            own_shares = lax.dynamic_slice_in_dim(
                shares_block, lax.axis_index("var") * share_width, share_width, 1
            )
            own_freqs = lax.dynamic_slice_in_dim(
                freqs_block, lax.axis_index("smp") * freq_width, freq_width, 1
            )
    return (own_shares, own_freqs)


def solution(mesh):
    placed = (P("smp", "var"), P(None, ("smp", "var")), P(None, ("var", "smp")))
    return jax.shard_map(
        body,
        mesh=mesh,
        in_specs=placed,
        out_specs=(P(None, ("smp", "var")), P(None, ("var", "smp"))),
        check_vma=False,
    )
```

profile of v0, /device:TPU:0, one launch (start us, length us, event | category | flops | bytes accessed | tf_op | source)
XLA Modules:
  0.0 156.3 jit_solution(4070201371241163746)
XLA Ops:
  0.6 0.8 reduce_sum.27
  1.4 6.2 %all_gather.6 = f32[12,1024]{1,0:T(8,128)S(1)} all-gather(f32[12,256]{1,0:T(8,128)S(1)} %broadcast_divide_fusion), channel_id=1, replica_groups=mesh['smp'=8,'var'=4] {'var'}, dimensions={1}, use_global_device_ids=true | all-gather | bytes 61440 | tf_op jit(solution)/shard_map/all_gather | solution.py:64
  7.7 0.0 copy-start.2
  7.7 0.7 copy-done.2
  8.4 31.4 %all-gather = f32[8,64,12]{1,2,0:T(8,128)S(1)} all-gather(f32[1,64,12]{1,2,0:T(8,128)S(1)} %bitcast.171), channel_id=1, replica_groups=mesh['smp'=8,'var'=4] {'smp'}, dimensions={0}, use_global_device_ids=true | all-gather | bytes 27648 | tf_op jit(solution)/shard_map/all_gather | solution.py:65
  39.8 0.1 reshape.53
  39.9 0.8 copy-done
  40.7 10.8 %while.30 = (s32[]{:T(128)}, f32[12,512]{1,0:T(8,128)S(1)}, f32[12,512]{1,0:T(8,128)S(1)}, f32[4,12,256]{2,1,0:T(8,128)S(1)}, f32[4,12,256]{2,1,0:T(8,128)S(1)},...) while((s32[]{:T(128)}, f32[12,512]{1,0:T(8,128)S(1)}, ...), condition=%wide.region_2.3_spmd.clone, body=%wide.region_1.2_spmd.clone.sunk | while | flops 95716368 | bytes 3547396 | solution.py:43
  40.7 0.1 shift_right_arithmetic.118
  40.8 0.8 fusion.92
  41.6 0.4 convolution_add_fusion.10
  41.9 0.4 convolution_add_fusion.11
  42.3 0.5 convolution_bitcast_fusion.4
  42.8 0.5 fusion.93
  43.4 0.1 shift_right_arithmetic.118
  43.5 0.8 fusion.92
  44.2 0.4 convolution_add_fusion.10
  44.6 0.4 convolution_add_fusion.11
  45.0 0.5 convolution_bitcast_fusion.4
  45.5 0.5 fusion.93
  46.1 0.1 shift_right_arithmetic.118
  46.2 0.8 fusion.92
  46.9 0.4 convolution_add_fusion.10
  47.3 0.4 convolution_add_fusion.11
  47.7 0.5 convolution_bitcast_fusion.4
  48.2 0.5 fusion.93
  48.8 0.1 shift_right_arithmetic.118
  48.8 0.8 fusion.92
  49.6 0.4 convolution_add_fusion.10
  50.0 0.4 convolution_add_fusion.11
  50.4 0.5 convolution_bitcast_fusion.4
  50.9 0.5 fusion.93
  51.5 10.7 %psum.42 = f32[12,1024]{1,0:T(8,128)S(1)} all-reduce(f32[12,1024]{1,0:T(8,128)S(1)} %bitcast.169), channel_id=1, replica_groups=mesh['smp'=8,'var'=4] {'var'}, use_global_device_ids=true, to_apply=%region_3.4 | all-reduce | flops 12288 | bytes 98304 | tf_op jit(solution)/shard_map/psum | solution.py:68
  62.3 37.5 %all-reduce.1 = (f32[12,512]{1,0:T(8,128)S(1)}, f32[12,512]{1,0:T(8,128)S(1)}) all-reduce(f32[12,512]{1,0:T(8,128)S(1)} %get-tuple-element.82, f32[12,512]{1,0:T(8,128)S(1)} %get-tuple-element.81), channel_id=1, replica_groups=mesh['smp'=8,'var'=4] {'smp'}, use_global_device_ids=true, to_apply=%region_6.7 | all-reduce | flops 12288 | bytes 98304 | tf_op jit(solution)/shard_map/psum | solution.py:69
  99.9 10.8 %while.31 = (s32[]{:T(128)}, f32[12,512]{1,0:T(8,128)S(1)}, f32[12,512]{1,0:T(8,128)S(1)}, f32[4,12,256]{2,1,0:T(8,128)S(1)}, f32[4,12,256]{2,1,0:T(8,128)S(1)},...) while((s32[]{:T(128)}, f32[12,512]{1,0:T(8,128)S(1)}, ...), condition=%wide.region_8.9_spmd.clone, body=%wide.region_7.8_spmd.clone.sunk | while | flops 95716368 | bytes 3547396 | solution.py:43
  99.9 0.1 shift_right_arithmetic.123
  100.0 0.8 fusion.103
  100.8 0.4 convolution_add_fusion.12
  101.2 0.4 convolution_add_fusion.13
  101.5 0.5 convolution_bitcast_fusion.5
  102.1 0.5 fusion.104
  102.6 0.1 shift_right_arithmetic.123
  102.7 0.8 fusion.103
  103.5 0.4 convolution_add_fusion.12
  103.9 0.4 convolution_add_fusion.13
  104.2 0.5 convolution_bitcast_fusion.5
  104.8 0.5 fusion.104
  105.3 0.1 shift_right_arithmetic.123
  105.4 0.8 fusion.103
  106.2 0.4 convolution_add_fusion.12
  106.6 0.4 convolution_add_fusion.13
  106.9 0.5 convolution_bitcast_fusion.5
  107.5 0.5 fusion.104
  108.0 0.1 shift_right_arithmetic.123
  108.1 0.8 fusion.103
  108.9 0.4 convolution_add_fusion.12
  109.3 0.4 convolution_add_fusion.13
  109.6 0.5 convolution_bitcast_fusion.5
  110.2 0.5 fusion.104
  110.8 10.7 %psum.45 = f32[12,1024]{1,0:T(8,128)S(1)} all-reduce(f32[12,1024]{1,0:T(8,128)S(1)} %bitcast.170), channel_id=1, replica_groups=mesh['smp'=8,'var'=4] {'var'}, use_global_device_ids=true, to_apply=%region_9.10 | all-reduce | flops 12288 | bytes 98304 | tf_op jit(solution)/shard_map/psum | solution.py:68
  121.5 0.1 dynamic-slice
  121.6 0.6 fusion.44
  122.2 33.4 %all-reduce = (f32[12,512]{1,0:T(8,128)S(1)}, f32[12,512]{1,0:T(8,128)S(1)}) all-reduce(f32[12,512]{1,0:T(8,128)S(1)} %get-tuple-element.85, f32[12,512]{1,0:T(8,128)S(1)} %get-tuple-element.84), channel_id=1, replica_groups=mesh['smp'=8,'var'=4] {'smp'}, use_global_device_ids=true, to_apply=%region_12.13 | all-reduce | flops 12288 | bytes 98304 | tf_op jit(solution)/shard_map/psum | solution.py:69
  155.6 0.7 fusion.47
  (51 shorter events, 0.5 us)
Async XLA Ops:
  0.6 0.8 copy-start.1
  7.7 0.7 copy-start.2
  39.8 0.9 copy-start
where the time goes:
time: 157 us; the launch traced here: 156 us
  blocking collectives  130 us (83%)
  matrix products  20.5 us (13%)
  local copies, waits for them, and re-layouts  2.55 us (2%)
  other arithmetic  2.3 us (1%)
    psum x2, blocking collectives, body(): sum_a, sum_b = lax.psum((part_a, part_b), 'smp')  70.9 us
    all_gather x1, blocking collectives, body(): freqs_block = lax.all_gather(own_freqs, 'smp', axis=1, tiled=True)  31.4 us
    psum x2, blocking collectives, body(): sum_q = lax.psum(part_q, 'var')  21.3 us
    dot_general x8, matrix products, expect_sums(): probs = jnp.einsum('kn,km->nm', shares_block, freqs_block, precision=HIGH)  6.22 us
    all_gather x1, blocking collectives, body(): shares_block = lax.all_gather(own_shares, 'var', axis=1, tiled=True)  6.22 us
    dot_general x8, matrix products, expect_sums(): jnp.einsum('km,nm->kn', 1.0 - freqs_block, ratio_ref, precision=HIGH)  4.22 us
    dot_general x8, matrix products, expect_sums(): jnp.einsum('km,nm->kn', freqs_block, ratio_alt, precision=HIGH)  4.14 us

commit v1 on v0

--- a/solution.py
+++ b/solution.py
@@ -65,7 +65,9 @@
     freqs_block = lax.all_gather(own_freqs, "smp", axis=1, tiled=True)
     for iteration in range(ITERS):
         part_q, part_a, part_b = block_sums(dosage, shares_block, freqs_block)
-        sum_q = lax.psum(part_q, "var")
+        sum_q = part_q
+        for hop in (1, 2):
+            sum_q = sum_q + lax.ppermute(sum_q, "var", [(dev, dev ^ hop) for dev in range(4)])
         sum_a, sum_b = lax.psum((part_a, part_b), "smp")
         shares_block = renew_shares(shares_block, sum_q)
         freqs_block = renew_freqs(freqs_block, sum_a, sum_b)

time: 157 us -> 143 us (0.911)
  blocking collectives: 130 us -> 108 us
  waiting for transfers between devices: 0 us -> 4.84 us
  starting transfers between devices: 0 us -> 3.25 us
    psum x2 -> x0, blocking collectives: 21.3 us -> none  [body(): sum_q = lax.psum(part_q, 'var')]
    ppermute x0 -> x4, waiting for transfers between devices: none -> 4.84 us  [body(): lax.ppermute(sum_q, 'var', [(dev, dev ^ hop) for dev in range(4)])]
    ppermute x0 -> x4, starting transfers between devices: none -> 3.25 us  [body(): lax.ppermute(sum_q, 'var', [(dev, dev ^ hop) for dev in range(4)])]
  transfers between devices with their start and end apart: 0 -> 4, of which waited for: 0 -> 2; matrix products, arithmetic and copies ran while one was open for 0% -> 0% of each run, Pallas kernels for 0% -> 0%
where the time goes in v1:
time: 143 us
  blocking collectives  108 us (76%)
  matrix products  20.5 us (14%)
  waiting for transfers between devices  4.84 us (3%)
  starting transfers between devices  3.25 us (2%)
  local copies, waits for them, and re-layouts  2.55 us (2%)
  other arithmetic  2.3 us (2%)
    psum x2, blocking collectives, body(): sum_a, sum_b = lax.psum((part_a, part_b), 'smp')  70.9 us
    all_gather x1, blocking collectives, body(): freqs_block = lax.all_gather(own_freqs, 'smp', axis=1, tiled=True)  31.4 us
    dot_general x8, matrix products, expect_sums(): probs = jnp.einsum('kn,km->nm', shares_block, freqs_block, precision=HIGH)  6.22 us
    all_gather x1, blocking collectives, body(): shares_block = lax.all_gather(own_shares, 'var', axis=1, tiled=True)  6.22 us
    ppermute x4, waiting for transfers between devices, body(): lax.ppermute(sum_q, 'var', [(dev, dev ^ hop) for dev in range(4)])  4.84 us
    dot_general x8, matrix products, expect_sums(): jnp.einsum('km,nm->kn', 1.0 - freqs_block, ratio_ref, precision=HIGH)  4.22 us
    dot_general x8, matrix products, expect_sums(): jnp.einsum('km,nm->kn', freqs_block, ratio_alt, precision=HIGH)  4.14 us
    ppermute x4, starting transfers between devices, body(): lax.ppermute(sum_q, 'var', [(dev, dev ^ hop) for dev in range(4)])  3.25 us
  transfers between devices with their start and end apart: 4, of which 2 were waited for; matrix products, arithmetic and copies ran while one was open for 0% of the time, Pallas kernels for 0%

profile of v1, /device:TPU:0, one launch (start us, length us, event | category | flops | bytes accessed | tf_op | source)
XLA Modules:
  0.0 143.1 jit_solution(13478180852487959215)
XLA Ops:
  0.7 0.8 reduce_sum.27
  1.5 6.2 %all_gather.6 = f32[12,1024]{1,0:T(8,128)S(1)} all-gather(f32[12,256]{1,0:T(8,128)S(1)} %broadcast_divide_fusion), channel_id=1, replica_groups=mesh['smp'=8,'var'=4] {'var'}, dimensions={1}, use_global_device_ids=true | all-gather | bytes 61440 | tf_op jit(solution)/shard_map/all_gather | solution.py:64
  7.7 0.7 copy-done.2
  8.4 31.4 %all-gather = f32[8,64,12]{1,2,0:T(8,128)S(1)} all-gather(f32[1,64,12]{1,2,0:T(8,128)S(1)} %bitcast.173), channel_id=1, replica_groups=mesh['smp'=8,'var'=4] {'smp'}, dimensions={0}, use_global_device_ids=true | all-gather | bytes 27648 | tf_op jit(solution)/shard_map/all_gather | solution.py:65
  39.9 0.8 copy-done
  40.7 10.8 %while.30 = (s32[]{:T(128)}, f32[12,512]{1,0:T(8,128)S(1)}, f32[12,512]{1,0:T(8,128)S(1)}, f32[4,12,256]{2,1,0:T(8,128)S(1)}, f32[4,12,256]{2,1,0:T(8,128)S(1)},...) while((s32[]{:T(128)}, f32[12,512]{1,0:T(8,128)S(1)}, ...), condition=%wide.region_2.3_spmd.clone, body=%wide.region_1.2_spmd.clone.sunk | while | flops 95716368 | bytes 3547396 | solution.py:43
  40.7 0.1 shift_right_arithmetic.118
  40.8 0.8 fusion.93
  41.6 0.4 convolution_add_fusion.10
  41.9 0.4 convolution_add_fusion.11
  42.3 0.5 convolution_bitcast_fusion.4
  42.8 0.5 fusion.94
  43.4 0.1 shift_right_arithmetic.118
  43.5 0.8 fusion.93
  44.2 0.4 convolution_add_fusion.10
  44.6 0.4 convolution_add_fusion.11
  45.0 0.5 convolution_bitcast_fusion.4
  45.5 0.5 fusion.94
  46.1 0.1 shift_right_arithmetic.118
  46.2 0.8 fusion.93
  46.9 0.4 convolution_add_fusion.10
  47.3 0.4 convolution_add_fusion.11
  47.7 0.5 convolution_bitcast_fusion.4
  48.2 0.5 fusion.94
  48.8 0.1 shift_right_arithmetic.118
  48.8 0.8 fusion.93
  49.6 0.4 convolution_add_fusion.10
  50.0 0.4 convolution_add_fusion.11
  50.4 0.5 convolution_bitcast_fusion.4
  50.9 0.5 fusion.94
  51.6 37.5 %all-reduce.1 = (f32[12,512]{1,0:T(8,128)S(1)}, f32[12,512]{1,0:T(8,128)S(1)}) all-reduce(f32[12,512]{1,0:T(8,128)S(1)} %get-tuple-element.82, f32[12,512]{1,0:T(8,128)S(1)} %get-tuple-element.81), channel_id=1, replica_groups=mesh['smp'=8,'var'=4] {'smp'}, use_global_device_ids=true, to_apply=%region_5.6 | all-reduce | flops 12288 | bytes 98304 | tf_op jit(solution)/shard_map/psum | solution.py:71
  89.2 1.6 %collective-permute-start.1 = (f32[12,1024]{1,0:T(8,128)S(1)}, f32[12,1024]{1,0:T(8,128)S(1)}, u32[]{:S(2)}, u32[]{:S(2)}) collective-permute-start(f32[12,1024]{1,0:T(8,128)S(1)} %add.90), channel_id=1, source_target_pairs={{0,2},{1,3},{2,0},{3,1},{4,6},{5,7},{6,4},{7,5},{8,10},{9,11},{10,... | collective-permute-start | bytes 147464 | tf_op jit(solution)/shard_map/ppermute | solution.py:70
  90.8 2.7 %collective-permute-done.1 = f32[12,1024]{1,0:T(8,128)S(1)} collective-permute-done((f32[12,1024]{1,0:T(8,128)S(1)}, f32[12,1024]{1,0:T(8,128)S(1)}, u32[]{:S(2)}, u32[]{:S(2)}) %collective-permute-start.1) | collective-permute-done | bytes 49184 | tf_op jit(solution)/shard_map/ppermute | solution.py:70
  93.6 10.8 %while.31 = (s32[]{:T(128)}, f32[12,512]{1,0:T(8,128)S(1)}, f32[12,512]{1,0:T(8,128)S(1)}, f32[4,12,256]{2,1,0:T(8,128)S(1)}, f32[4,12,256]{2,1,0:T(8,128)S(1)},...) while((s32[]{:T(128)}, f32[12,512]{1,0:T(8,128)S(1)}, ...), condition=%wide.region_7.8_spmd.clone, body=%wide.region_6.7_spmd.clone.sunk | while | flops 95716368 | bytes 3547396 | solution.py:43
  93.7 0.1 shift_right_arithmetic.123
  93.7 0.8 fusion.104
  94.5 0.4 convolution_add_fusion.12
  94.9 0.4 convolution_add_fusion.13
  95.3 0.5 convolution_bitcast_fusion.5
  95.8 0.5 fusion.105
  96.3 0.1 shift_right_arithmetic.123
  96.4 0.8 fusion.104
  97.2 0.4 convolution_add_fusion.12
  97.6 0.4 convolution_add_fusion.13
  98.0 0.5 convolution_bitcast_fusion.5
  98.5 0.5 fusion.105
  99.0 0.1 shift_right_arithmetic.123
  99.1 0.8 fusion.104
  99.9 0.4 convolution_add_fusion.12
  100.3 0.4 convolution_add_fusion.13
  100.7 0.5 convolution_bitcast_fusion.5
  101.2 0.5 fusion.105
  101.7 0.1 shift_right_arithmetic.123
  101.8 0.8 fusion.104
  102.6 0.4 convolution_add_fusion.12
  103.0 0.4 convolution_add_fusion.13
  103.4 0.5 convolution_bitcast_fusion.5
  103.9 0.5 fusion.105
  104.6 33.4 %all-reduce = (f32[12,512]{1,0:T(8,128)S(1)}, f32[12,512]{1,0:T(8,128)S(1)}) all-reduce(f32[12,512]{1,0:T(8,128)S(1)} %get-tuple-element.85, f32[12,512]{1,0:T(8,128)S(1)} %get-tuple-element.84), channel_id=1, replica_groups=mesh['smp'=8,'var'=4] {'smp'}, use_global_device_ids=true, to_apply=%region_10.11 | all-reduce | flops 12288 | bytes 98304 | tf_op jit(solution)/shard_map/psum | solution.py:71
  138.0 1.6 %collective-permute-start.3 = (f32[12,1024]{1,0:T(8,128)S(1)}, f32[12,1024]{1,0:T(8,128)S(1)}, u32[]{:S(2)}, u32[]{:S(2)}) collective-permute-start(f32[12,1024]{1,0:T(8,128)S(1)} %add.97), channel_id=1, source_target_pairs={{0,2},{1,3},{2,0},{3,1},{4,6},{5,7},{6,4},{7,5},{8,10},{9,11},{10,... | collective-permute-start | bytes 147464 | tf_op jit(solution)/shard_map/ppermute | solution.py:70
  139.6 0.7 fusion.47
  140.3 2.1 %collective-permute-done.3 = f32[12,1024]{1,0:T(8,128)S(1)} collective-permute-done((f32[12,1024]{1,0:T(8,128)S(1)}, f32[12,1024]{1,0:T(8,128)S(1)}, u32[]{:S(2)}, u32[]{:S(2)}) %collective-permute-start.3) | collective-permute-done | bytes 49184 | tf_op jit(solution)/shard_map/ppermute | solution.py:70
  142.4 0.1 dynamic-slice
  142.5 0.6 fusion.44
  (59 shorter events, 0.7 us)
Async XLA Ops:
  0.6 0.8 copy-start.1
  7.7 0.7 copy-start.2
  39.8 0.9 copy-start
  51.5 37.6 %collective-permute-start = (f32[12,1024]{1,0:T(8,128)S(1)}, f32[12,1024]{1,0:T(8,128)S(1)}, u32[]{:S(2)}, u32[]{:S(2)}) collective-permute-start(f32[12,1024]{1,0:T(8,128)S(1)} %bitcast.167), channel_id=1, source_target_pairs={{0,1},{1,0},{2,3},{3,2},{4,5},{5,4},{6,7},{7,6},{8,9},{9,8},{10,11... | collective-permute-start | bytes 147464 | tf_op jit(solution)/shard_map/ppermute | solution.py:70
  89.2 4.3 %collective-permute-start.1 = (f32[12,1024]{1,0:T(8,128)S(1)}, f32[12,1024]{1,0:T(8,128)S(1)}, u32[]{:S(2)}, u32[]{:S(2)}) collective-permute-start(f32[12,1024]{1,0:T(8,128)S(1)} %add.90), channel_id=1, source_target_pairs={{0,2},{1,3},{2,0},{3,1},{4,6},{5,7},{6,4},{7,5},{8,10},{9,11},{10,... | collective-permute-start | bytes 147464 | tf_op jit(solution)/shard_map/ppermute | solution.py:70
  104.5 33.5 %collective-permute-start.2 = (f32[12,1024]{1,0:T(8,128)S(1)}, f32[12,1024]{1,0:T(8,128)S(1)}, u32[]{:S(2)}, u32[]{:S(2)}) collective-permute-start(f32[12,1024]{1,0:T(8,128)S(1)} %bitcast.165), channel_id=1, source_target_pairs={{0,1},{1,0},{2,3},{3,2},{4,5},{5,4},{6,7},{7,6},{8,9},{9,8},{10,11... | collective-permute-start | bytes 147464 | tf_op jit(solution)/shard_map/ppermute | solution.py:70
  138.0 4.3 %collective-permute-start.3 = (f32[12,1024]{1,0:T(8,128)S(1)}, f32[12,1024]{1,0:T(8,128)S(1)}, u32[]{:S(2)}, u32[]{:S(2)}) collective-permute-start(f32[12,1024]{1,0:T(8,128)S(1)} %add.97), channel_id=1, source_target_pairs={{0,2},{1,3},{2,0},{3,1},{4,6},{5,7},{6,4},{7,5},{8,10},{9,11},{10,... | collective-permute-start | bytes 147464 | tf_op jit(solution)/shard_map/ppermute | solution.py:70
